TPU v7x, 32 devices: a whole 2x2x4 slice. The times are simulated.
32 devices in a mesh: row: 8 (over z, y), col: 4 (over x, core).
Axes of the slice: x: 2, y: 2, z: 4, core: 2. Of those that a mesh axis runs over, the one named last changes fastest.
Arguments:
- weights: float32 [2, 4, 2048, 8, 1024], P(None, None, 'row', None, 'col'), may hold values from -6 to 6
Outputs:
- trailing: float32 [2, 4, 2048, 8, 1024], P(None, None, 'row', None, 'col')
- diagonal: float32 [2, 12], replicated
- superdiag: float32 [2, 12], replicated
All inputs are finite; a program needn't handle non-finite values.
Results may differ from a plain program's by a relative error of at most 0.0003.
Values sent between devices are 32-bit elements; how exact they have to be, the bound alone decides.
A program may use at most 128 MiB of HBM per device.

v0:
```python
import jax
import jax.numpy as jnp
from jax import lax
from jax.sharding import PartitionSpec as P

STEPS = 6
PANELS = 2


def broadcast(block, axis, owner):
    block = jnp.where(lax.axis_index(axis) == owner, block, jnp.zeros_like(block))
    return lax.psum(block, axis)


def contract(form, left, right):
    return jnp.einsum(form, left, right, precision=lax.Precision.HIGHEST)


def reflect(leading, squares):
    length = jnp.sqrt(squares)
    divisor = jnp.maximum(leading + length, 1.0)
    factor = (leading + length) / jnp.maximum(length, 1.0)
    return (divisor, factor, -length)


def placed(global_at, devices, tile_len):
    owner = global_at // tile_len % devices
    local_at = global_at // (devices * tile_len) * tile_len + global_at % tile_len
    return (owner, local_at)


def panel_merged(
    mats, grow, gcol, first_at, row_devices, col_devices, tile_len, row_place, col_place
):
    batch_n, local_rows, local_cols = mats.shape
    col_refl = jnp.zeros((batch_n, STEPS, local_rows), jnp.float32)
    col_aux = jnp.zeros((batch_n, STEPS, local_rows), jnp.float32)
    row_aux = jnp.zeros((batch_n, STEPS, local_cols), jnp.float32)
    row_refl = jnp.zeros((batch_n, STEPS, local_cols), jnp.float32)
    diag_list = []
    super_list = []
    start_owner, start_local = placed(first_at, col_devices, tile_len)
    pivot_col = broadcast(mats[:, :, start_local], "col", start_owner)
    aux_at = jnp.zeros((batch_n, STEPS), jnp.float32)
    refl_at = jnp.zeros((batch_n, STEPS), jnp.float32)
    for step_at in range(STEPS):
        pivot = first_at + step_at
        row_owner, row_local = placed(pivot, row_devices, tile_len)
        next_owner, next_local = placed(pivot + 1, col_devices, tile_len)
        col_piece = (
            pivot_col
            - contract("mp,mpr->mr", aux_at, col_refl)
            - contract("mp,mpr->mr", refl_at, col_aux)
        )
        col_piece = jnp.where(grow >= pivot, col_piece, 0.0)
        own_row = row_place == row_owner
        summed = lax.psum(
            (
                contract("mrc,mr->mc", mats, col_piece),
                contract("mpr,mr->mp", col_refl, col_piece),
                contract("mpr,mr->mp", col_aux, col_piece),
                jnp.sum(col_piece * col_piece, axis=1),
                jnp.sum(jnp.where(grow == pivot, col_piece, 0.0), axis=1),
                jnp.where(own_row, mats[:, row_local, :], 0.0),
                jnp.where(own_row, col_refl[:, :, row_local], 0.0),
                jnp.where(own_row, col_aux[:, :, row_local], 0.0),
            ),
            "row",
        )
        trans_piece, refl_dots, aux_dots, squares, leading, pivot_row, refl_row, aux_row = summed
        divisor, factor, bidiag = reflect(leading, squares)
        remain = (1.0 - leading / divisor)[:, None]
        col_vec = jnp.where(grow == pivot, 1.0, col_piece / divisor[:, None])
        transposed = trans_piece / divisor[:, None] + pivot_row * remain
        weighs_one = refl_dots / divisor[:, None] + refl_row * remain
        weighs_two = aux_dots / divisor[:, None] + aux_row * remain
        col_refl = col_refl.at[:, step_at].set(col_vec)
        col_img = factor[:, None] * (
            transposed
            - contract("mp,mpc->mc", weighs_one, row_aux)
            - contract("mp,mpc->mc", weighs_two, row_refl)
        )
        col_img = jnp.where(gcol > pivot, col_img, 0.0)
        row_aux = row_aux.at[:, step_at].set(col_img)
        refl_row = refl_row.at[:, step_at].set(1.0)
        row_piece = (
            pivot_row
            - contract("mp,mpc->mc", refl_row, row_aux)
            - contract("mp,mpc->mc", aux_row, row_refl)
        )
        row_piece = jnp.where(gcol > pivot, row_piece, 0.0)
        own_col = col_place == next_owner
        gathered = lax.psum(
            (
                contract("mrc,mc->mr", mats, row_piece),
                contract("mpc,mc->mp", row_aux, row_piece),
                contract("mpc,mc->mp", row_refl, row_piece),
                jnp.sum(row_piece * row_piece, axis=1),
                jnp.sum(jnp.where(gcol == pivot + 1, row_piece, 0.0), axis=1),
                jnp.where(own_col, mats[:, :, next_local], 0.0),
                jnp.where(own_col, row_aux[:, :, next_local], 0.0),
                jnp.where(own_col, row_refl[:, :, next_local], 0.0),
            ),
            "col",
        )
        apply_piece, aux_proj, refl_proj, squares2, leading2, next_col, next_aux, next_refl = (
            gathered
        )
        divisor2, factor2, bidiag2 = reflect(leading2, squares2)
        remain2 = (1.0 - leading2 / divisor2)[:, None]
        row_vec = jnp.where(gcol == pivot + 1, 1.0, row_piece / divisor2[:, None])
        applied = apply_piece / divisor2[:, None] + next_col * remain2
        dots_one = aux_proj / divisor2[:, None] + next_aux * remain2
        dots_two = refl_proj / divisor2[:, None] + next_refl * remain2
        row_refl = row_refl.at[:, step_at].set(row_vec)
        row_img = factor2[:, None] * (
            applied
            - contract("mp,mpr->mr", dots_one, col_refl)
            - contract("mp,mpr->mr", dots_two, col_aux)
        )
        row_img = jnp.where(grow > pivot, row_img, 0.0)
        col_aux = col_aux.at[:, step_at].set(row_img)
        diag_list.append(bidiag)
        super_list.append(bidiag2)
        pivot_col = next_col
        aux_at = next_aux
        refl_at = next_refl.at[:, step_at].set(1.0)
    return (col_refl, col_aux, row_aux, row_refl, diag_list, super_list)


def per_device(weights):
    batch_n, row_cycles, tile_len, col_cycles, _ = weights.shape
    local_rows = row_cycles * tile_len
    local_cols = col_cycles * tile_len
    mats = weights.reshape(batch_n, local_rows, local_cols)
    row_devices = lax.axis_size("row")
    col_devices = lax.axis_size("col")
    row_place = lax.axis_index("row")
    col_place = lax.axis_index("col")
    row_ids = jnp.arange(local_rows, dtype=jnp.int32)
    col_ids = jnp.arange(local_cols, dtype=jnp.int32)
    grow = (
        row_ids // tile_len * (row_devices * tile_len) + row_place * tile_len + row_ids % tile_len
    )
    gcol = (
        col_ids // tile_len * (col_devices * tile_len) + col_place * tile_len + col_ids % tile_len
    )
    diag_all = []
    super_all = []
    for panel_at in range(PANELS):
        first_at = panel_at * STEPS
        result = panel_merged(
            mats, grow, gcol, first_at, row_devices, col_devices, tile_len, row_place, col_place
        )
        col_refl, col_aux, row_aux, row_refl, diag_list, super_list = result
        mats = (
            mats
            - contract("mpr,mpc->mrc", col_refl, row_aux)
            - contract("mpr,mpc->mrc", col_aux, row_refl)
        )
        diag_all = diag_all + diag_list
        super_all = super_all + super_list
    done = PANELS * STEPS
    inside = (grow[:, None] >= done) & (gcol[None, :] >= done)
    trailing = jnp.where(inside[None], mats, 0.0).reshape(weights.shape)
    return (trailing, jnp.stack(diag_all, axis=1), jnp.stack(super_all, axis=1))


def solution(mesh):
    placed = (P(None, None, "row", None, "col"),)
    return jax.shard_map(
        per_device,
        mesh=mesh,
        in_specs=placed,
        out_specs=(P(None, None, "row", None, "col"), P(), P()),
        check_vma=False,
    )
```

profile of v0, /device:TPU:0, one launch (start us, length us, event | category | flops | bytes accessed | tf_op | source)
XLA Modules:
  0.0 1119.1 jit_solution(389698019643860435)
XLA Ops:
  0.6 18.0 %reshape.2177 = f32[2,1024,2048]{2,1,0:T(8,128)} reshape(f32[2,4,256,8,256]{4,3,2,1,0:T(8,128)} %param.141) | data formatting | bytes 33554432 | tf_op jit(solution)/shard_map/reshape | solution.py:135
  35.3 11.5 %fusion.426 = f32[2,1,2048]{2,1,0:T(1,128)S(1)} fusion(f32[2,1024,2048]{2,1,0:T(8,128)} %reshape.2177, f32[2,1024,1]{1,0,2:T(2,128)S(1)} %bitcast.1338), kind=kOutput, calls=%fused_computation.717 | convolution fusion | flops 50331648 | bytes 16801792 | tf_op jit(solution)/shard_map/mrc,mr->mc/dot_general | solution.py:16
  48.5 38.2 %all-reduce.20 = (f32[2,6]{1,0:T(2,128)S(1)}, f32[2]{0:T(128)S(1)}, f32[2]{0:T(128)S(1)}, f32[2,2048]{1,0:T(2,128)S(1)}, f32[2,2048]{1,0:T(2,128)S(1)}) all-reduce(f32[2,6]{1,0:T(2,128)S(1)} %bitcast.1535, f32[2]{0:T(128)S(1)} %get-tuple-element.920, f32[2]{0:T(128)S(1)} %get-tuple-element.919, ...), channel_id=1, replica_groups=mesh['row'=8,'col'=4] {'row'}, use_global_device_ids=true, to_apply=%region_8.9 | all-reduce | flops 8208 | bytes 65664 | tf_op jit(solution)/shard_map/psum | solution.py:57
  89.2 17.1 %fusion.480 = f32[2,1,1024]{2,1,0:T(1,128)S(1)} fusion(f32[2,1024,2048]{2,1,0:T(8,128)} %reshape.2177, f32[2,2048,1]{1,0,2:T(2,128)S(1)} %bitcast.1287), kind=kOutput, calls=%fused_computation.900 | convolution fusion | flops 50331648 | bytes 16801792 | tf_op jit(solution)/shard_map/mrc,mc->mr/dot_general | solution.py:16
  107.2 11.0 all-reduce.32
  120.0 11.5 %fusion.520 = f32[2,1,2048]{2,1,0:T(1,128)S(1)} fusion(f32[2,1024,2048]{2,1,0:T(8,128)} %reshape.2177, f32[2,1024,1]{1,0,2:T(2,128)S(1)} %bitcast.1310), kind=kOutput, calls=%fused_computation.1013 | convolution fusion | flops 50331648 | bytes 16801792 | tf_op jit(solution)/shard_map/mrc,mr->mc/dot_general | solution.py:16
  131.9 33.4 %all-reduce.19 = (f32[2,2048]{1,0:T(2,128)S(1)}, f32[2,6]{1,0:T(2,128)S(1)}, f32[2,6]{1,0:T(2,128)S(1)}, f32[2]{0:T(128)S(1)}, f32[2]{0:T(128)S(1)}, /*index=5*/...) all-reduce(f32[2,2048]{1,0:T(2,128)S(1)} %bitcast.1342, ...), channel_id=1, replica_groups=mesh['row'=8,'col'=4] {'row'}, use_global_device_ids=true, to_apply=%region_23.24 | all-reduce | flops 8244 | bytes 65952 | tf_op jit(solution)/shard_map/psum | solution.py:57
  169.5 17.1 %fusion.472 = f32[2,1,1024]{2,1,0:T(1,128)S(1)} fusion(f32[2,1024,2048]{2,1,0:T(8,128)} %reshape.2177, f32[2,2048,1]{1,0,2:T(2,128)S(1)} %bitcast.1274), kind=kOutput, calls=%fused_computation.892 | convolution fusion | flops 50331648 | bytes 16801792 | tf_op jit(solution)/shard_map/mrc,mc->mr/dot_general | solution.py:16
  199.9 11.5 %fusion.516 = f32[2,1,2048]{2,1,0:T(1,128)S(1)} fusion(f32[2,1024,2048]{2,1,0:T(8,128)} %reshape.2177, f32[2,1024,1]{1,0,2:T(2,128)S(1)} %bitcast.1313), kind=kOutput, calls=%fused_computation.1009 | convolution fusion | flops 50331648 | bytes 16801792 | tf_op jit(solution)/shard_map/mrc,mr->mc/dot_general | solution.py:16
  211.7 35.3 %all-reduce.18 = (f32[2,2048]{1,0:T(2,128)S(1)}, f32[2,6]{1,0:T(2,128)S(1)}, f32[2,6]{1,0:T(2,128)S(1)}, f32[2]{0:T(128)S(1)}, f32[2]{0:T(128)S(1)}, /*index=5*/...) all-reduce(f32[2,2048]{1,0:T(2,128)S(1)} %bitcast.1346, ...), channel_id=1, replica_groups=mesh['row'=8,'col'=4] {'row'}, use_global_device_ids=true, to_apply=%region_44.45 | all-reduce | flops 8244 | bytes 65952 | tf_op jit(solution)/shard_map/psum | solution.py:57
  251.4 17.1 %fusion.468 = f32[2,1,1024]{2,1,0:T(1,128)S(1)} fusion(f32[2,1024,2048]{2,1,0:T(8,128)} %reshape.2177, f32[2,2048,1]{1,0,2:T(2,128)S(1)} %bitcast.1277), kind=kOutput, calls=%fused_computation.888 | convolution fusion | flops 50331648 | bytes 16801792 | tf_op jit(solution)/shard_map/mrc,mc->mr/dot_general | solution.py:16
  268.8 10.3 all-reduce.30
  281.9 11.5 %fusion.512 = f32[2,1,2048]{2,1,0:T(1,128)S(1)} fusion(f32[2,1024,2048]{2,1,0:T(8,128)} %reshape.2177, f32[2,1024,1]{1,0,2:T(2,128)S(1)} %bitcast.1316), kind=kOutput, calls=%fused_computation.1005 | convolution fusion | flops 50331648 | bytes 16801792 | tf_op jit(solution)/shard_map/mrc,mr->mc/dot_general | solution.py:16
  293.7 33.4 %all-reduce.17 = (f32[2,2048]{1,0:T(2,128)S(1)}, f32[2,6]{1,0:T(2,128)S(1)}, f32[2,6]{1,0:T(2,128)S(1)}, f32[2]{0:T(128)S(1)}, f32[2]{0:T(128)S(1)}, /*index=5*/...) all-reduce(f32[2,2048]{1,0:T(2,128)S(1)} %bitcast.1347, ...), channel_id=1, replica_groups=mesh['row'=8,'col'=4] {'row'}, use_global_device_ids=true, to_apply=%region_65.66 | all-reduce | flops 8244 | bytes 65952 | tf_op jit(solution)/shard_map/psum | solution.py:57
  331.6 17.1 %fusion.464 = f32[2,1,1024]{2,1,0:T(1,128)S(1)} fusion(f32[2,1024,2048]{2,1,0:T(8,128)} %reshape.2177, f32[2,2048,1]{1,0,2:T(2,128)S(1)} %bitcast.1280), kind=kOutput, calls=%fused_computation.884 | convolution fusion | flops 50331648 | bytes 16801792 | tf_op jit(solution)/shard_map/mrc,mc->mr/dot_general | solution.py:16
  349.1 10.3 all-reduce.29
  361.9 11.5 %fusion.508 = f32[2,1,2048]{2,1,0:T(1,128)S(1)} fusion(f32[2,1024,2048]{2,1,0:T(8,128)} %reshape.2177, f32[2,1024,1]{1,0,2:T(2,128)S(1)} %bitcast.1319), kind=kOutput, calls=%fused_computation.1001 | convolution fusion | flops 50331648 | bytes 16801792 | tf_op jit(solution)/shard_map/mrc,mr->mc/dot_general | solution.py:16
  373.8 35.4 %all-reduce.16 = (f32[2,2048]{1,0:T(2,128)S(1)}, f32[2,6]{1,0:T(2,128)S(1)}, f32[2,6]{1,0:T(2,128)S(1)}, f32[2]{0:T(128)S(1)}, f32[2]{0:T(128)S(1)}, /*index=5*/...) all-reduce(f32[2,2048]{1,0:T(2,128)S(1)} %bitcast.1348, ...), channel_id=1, replica_groups=mesh['row'=8,'col'=4] {'row'}, use_global_device_ids=true, to_apply=%region_86.87 | all-reduce | flops 8244 | bytes 65952 | tf_op jit(solution)/shard_map/psum | solution.py:57
  413.6 17.1 %fusion.460 = f32[2,1,1024]{2,1,0:T(1,128)S(1)} fusion(f32[2,1024,2048]{2,1,0:T(8,128)} %reshape.2177, f32[2,2048,1]{1,0,2:T(2,128)S(1)} %bitcast.1283), kind=kOutput, calls=%fused_computation.880 | convolution fusion | flops 50331648 | bytes 16801792 | tf_op jit(solution)/shard_map/mrc,mc->mr/dot_general | solution.py:16
  444.0 11.5 %fusion.504 = f32[2,1,2048]{2,1,0:T(1,128)S(1)} fusion(f32[2,1024,2048]{2,1,0:T(8,128)} %reshape.2177, f32[2,1024,1]{1,0,2:T(2,128)S(1)} %bitcast.1307), kind=kOutput, calls=%fused_computation.997 | convolution fusion | flops 50331648 | bytes 16801792 | tf_op jit(solution)/shard_map/mrc,mr->mc/dot_general | solution.py:16
  455.9 33.4 %all-reduce.15 = (f32[2,2048]{1,0:T(2,128)S(1)}, f32[2,6]{1,0:T(2,128)S(1)}, f32[2,6]{1,0:T(2,128)S(1)}, f32[2]{0:T(128)S(1)}, f32[2]{0:T(128)S(1)}, /*index=5*/...) all-reduce(f32[2,2048]{1,0:T(2,128)S(1)} %bitcast.1345, ...), channel_id=1, replica_groups=mesh['row'=8,'col'=4] {'row'}, use_global_device_ids=true, to_apply=%region_106.107 | all-reduce | flops 8244 | bytes 65952 | tf_op jit(solution)/shard_map/psum | solution.py:57
  492.5 17.1 %fusion.456 = f32[2,1,1024]{2,1,0:T(1,128)S(1)} fusion(f32[2,1024,2048]{2,1,0:T(8,128)} %reshape.2177, f32[2,2048,1]{1,0,2:T(2,128)S(1)} %bitcast.1286), kind=kOutput, calls=%fused_computation.876 | convolution fusion | flops 50331648 | bytes 16801792 | tf_op jit(solution)/shard_map/mrc,mc->mr/dot_general | solution.py:16
  509.9 10.5 all-reduce.27
  521.2 16.0 %fusion.144 = f32[2,1024,2048]{2,1,0:T(8,128)} fusion(f32[2,6,2048]{2,0,1:T(2,128)S(1)} %bitcast_dynamic-update-slice_fusion.11, f32[2,6,1024]{2,0,1:T(2,128)S(1)} %constant_dynamic-update-slice_fusion.11), kind=kOutput, calls=%fused_computation.161 | convolution fusion | flops 301989888 | bytes 16924672 | tf_op jit(solution)/shard_map/mpr,mpc->mrc/dot_general | solution.py:16
  537.1 22.1 %subtract_subtract_fusion = f32[2,1024,2048]{2,1,0:T(8,128)} fusion(f32[2,1024,2048]{2,1,0:T(8,128)} %reshape.2177, f32[2,1024,2048]{2,1,0:T(8,128)} %fusion.144, f32[2,6,2048]{2,0,1:T(2,128)S(1)} %bitcast_dynamic-update-slice_fusion.10, f32[2,6,1024]{2,0,1:T(2,128)S(1)} %constant_dynamic-update-slice_fusion.10), kind=kOutput, calls=%fused_computation.1 | convolution fusion | flops 310378496 | bytes 50479104 | tf_op jit(solution)/shard_map/mpr,mpc->mrc/dot_general | solution.py:16
  573.6 12.3 %fusion.423 = f32[2,1,2048]{2,1,0:T(1,128)S(1)} fusion(f32[2,1024,2048]{2,1,0:T(8,128)} %subtract_subtract_fusion, f32[2,1024,1]{1,0,2:T(2,128)S(1)} %bitcast.1340), kind=kOutput, calls=%fused_computation.714 | convolution fusion | flops 50331648 | bytes 16801792 | tf_op jit(solution)/shard_map/mrc,mr->mc/dot_general | solution.py:16
  587.5 35.4 %all-reduce.14 = (f32[2,6]{1,0:T(2,128)S(1)}, f32[2]{0:T(128)S(1)}, f32[2]{0:T(128)S(1)}, f32[2,2048]{1,0:T(2,128)S(1)}, f32[2,2048]{1,0:T(2,128)S(1)}) all-reduce(f32[2,6]{1,0:T(2,128)S(1)} %bitcast.1538, f32[2]{0:T(128)S(1)} %get-tuple-element.908, f32[2]{0:T(128)S(1)} %get-tuple-element.907, ...), channel_id=1, replica_groups=mesh['row'=8,'col'=4] {'row'}, use_global_device_ids=true, to_apply=%region_130.131 | all-reduce | flops 8208 | bytes 65664 | tf_op jit(solution)/shard_map/psum | solution.py:57
  623.9 17.6 %fusion.476 = f32[2,1,1024]{2,1,0:T(1,128)S(1)} fusion(f32[2,1024,2048]{2,1,0:T(8,128)} %subtract_subtract_fusion, f32[2,2048,1]{1,0,2:T(2,128)S(1)} %bitcast.1320), kind=kOutput, calls=%fused_computation.896 | convolution fusion | flops 50331648 | bytes 16801792 | tf_op jit(solution)/shard_map/mrc,mc->mr/dot_general | solution.py:16
  642.4 10.7 all-reduce.26
  654.8 12.3 %fusion.500 = f32[2,1,2048]{2,1,0:T(1,128)S(1)} fusion(f32[2,1024,2048]{2,1,0:T(8,128)} %subtract_subtract_fusion, f32[2,1024,1]{1,0,2:T(2,128)S(1)} %bitcast.1328), kind=kOutput, calls=%fused_computation.993 | convolution fusion | flops 50331648 | bytes 16801792 | tf_op jit(solution)/shard_map/mrc,mr->mc/dot_general | solution.py:16
  667.4 33.4 %all-reduce.13 = (f32[2,2048]{1,0:T(2,128)S(1)}, f32[2,6]{1,0:T(2,128)S(1)}, f32[2,6]{1,0:T(2,128)S(1)}, f32[2]{0:T(128)S(1)}, f32[2]{0:T(128)S(1)}, /*index=5*/...) all-reduce(f32[2,2048]{1,0:T(2,128)S(1)} %bitcast.1343, ...), channel_id=1, replica_groups=mesh['row'=8,'col'=4] {'row'}, use_global_device_ids=true, to_apply=%region_144.145 | all-reduce | flops 8244 | bytes 65952 | tf_op jit(solution)/shard_map/psum | solution.py:57
  704.4 17.6 %fusion.452 = f32[2,1,1024]{2,1,0:T(1,128)S(1)} fusion(f32[2,1024,2048]{2,1,0:T(8,128)} %subtract_subtract_fusion, f32[2,2048,1]{1,0,2:T(2,128)S(1)} %bitcast.1295), kind=kOutput, calls=%fused_computation.872 | convolution fusion | flops 50331648 | bytes 16801792 | tf_op jit(solution)/shard_map/mrc,mc->mr/dot_general | solution.py:16
  735.3 12.3 %fusion.496 = f32[2,1,2048]{2,1,0:T(1,128)S(1)} fusion(f32[2,1024,2048]{2,1,0:T(8,128)} %subtract_subtract_fusion, f32[2,1024,1]{1,0,2:T(2,128)S(1)} %bitcast.1331), kind=kOutput, calls=%fused_computation.989 | convolution fusion | flops 50331648 | bytes 16801792 | tf_op jit(solution)/shard_map/mrc,mr->mc/dot_general | solution.py:16
  748.0 35.4 %all-reduce.12 = (f32[2,2048]{1,0:T(2,128)S(1)}, f32[2,6]{1,0:T(2,128)S(1)}, f32[2,6]{1,0:T(2,128)S(1)}, f32[2]{0:T(128)S(1)}, f32[2]{0:T(128)S(1)}, /*index=5*/...) all-reduce(f32[2,2048]{1,0:T(2,128)S(1)} %bitcast.1349, ...), channel_id=1, replica_groups=mesh['row'=8,'col'=4] {'row'}, use_global_device_ids=true, to_apply=%region_164.165 | all-reduce | flops 8244 | bytes 65952 | tf_op jit(solution)/shard_map/psum | solution.py:57
  787.0 17.6 %fusion.448 = f32[2,1,1024]{2,1,0:T(1,128)S(1)} fusion(f32[2,1024,2048]{2,1,0:T(8,128)} %subtract_subtract_fusion, f32[2,2048,1]{1,0,2:T(2,128)S(1)} %bitcast.1298), kind=kOutput, calls=%fused_computation.868 | convolution fusion | flops 50331648 | bytes 16801792 | tf_op jit(solution)/shard_map/mrc,mc->mr/dot_general | solution.py:16
  818.0 12.3 %fusion.492 = f32[2,1,2048]{2,1,0:T(1,128)S(1)} fusion(f32[2,1024,2048]{2,1,0:T(8,128)} %subtract_subtract_fusion, f32[2,1024,1]{1,0,2:T(2,128)S(1)} %bitcast.1334), kind=kOutput, calls=%fused_computation.985 | convolution fusion | flops 50331648 | bytes 16801792 | tf_op jit(solution)/shard_map/mrc,mr->mc/dot_general | solution.py:16
  830.6 33.4 %all-reduce.11 = (f32[2,2048]{1,0:T(2,128)S(1)}, f32[2,6]{1,0:T(2,128)S(1)}, f32[2,6]{1,0:T(2,128)S(1)}, f32[2]{0:T(128)S(1)}, f32[2]{0:T(128)S(1)}, /*index=5*/...) all-reduce(f32[2,2048]{1,0:T(2,128)S(1)} %bitcast.1350, ...), channel_id=1, replica_groups=mesh['row'=8,'col'=4] {'row'}, use_global_device_ids=true, to_apply=%region_184.185 | all-reduce | flops 8244 | bytes 65952 | tf_op jit(solution)/shard_map/psum | solution.py:57
  867.9 17.6 %fusion.444 = f32[2,1,1024]{2,1,0:T(1,128)S(1)} fusion(f32[2,1024,2048]{2,1,0:T(8,128)} %subtract_subtract_fusion, f32[2,2048,1]{1,0,2:T(2,128)S(1)} %bitcast.1301), kind=kOutput, calls=%fused_computation.864 | convolution fusion | flops 50331648 | bytes 16801792 | tf_op jit(solution)/shard_map/mrc,mc->mr/dot_general | solution.py:16
  898.6 12.3 %fusion.488 = f32[2,1,2048]{2,1,0:T(1,128)S(1)} fusion(f32[2,1024,2048]{2,1,0:T(8,128)} %subtract_subtract_fusion, f32[2,1024,1]{1,0,2:T(2,128)S(1)} %bitcast.1337), kind=kOutput, calls=%fused_computation.981 | convolution fusion | flops 50331648 | bytes 16801792 | tf_op jit(solution)/shard_map/mrc,mr->mc/dot_general | solution.py:16
  911.3 35.4 %all-reduce.10 = (f32[2,2048]{1,0:T(2,128)S(1)}, f32[2,6]{1,0:T(2,128)S(1)}, f32[2,6]{1,0:T(2,128)S(1)}, f32[2]{0:T(128)S(1)}, f32[2]{0:T(128)S(1)}, /*index=5*/...) all-reduce(f32[2,2048]{1,0:T(2,128)S(1)} %bitcast.1351, ...), channel_id=1, replica_groups=mesh['row'=8,'col'=4] {'row'}, use_global_device_ids=true, to_apply=%region_204.205 | all-reduce | flops 8244 | bytes 65952 | tf_op jit(solution)/shard_map/psum | solution.py:57
  950.4 17.6 %fusion.440 = f32[2,1,1024]{2,1,0:T(1,128)S(1)} fusion(f32[2,1024,2048]{2,1,0:T(8,128)} %subtract_subtract_fusion, f32[2,2048,1]{1,0,2:T(2,128)S(1)} %bitcast.1304), kind=kOutput, calls=%fused_computation.860 | convolution fusion | flops 50331648 | bytes 16801792 | tf_op jit(solution)/shard_map/mrc,mc->mr/dot_general | solution.py:16
  981.3 12.3 %fusion.484 = f32[2,1,2048]{2,1,0:T(1,128)S(1)} fusion(f32[2,1024,2048]{2,1,0:T(8,128)} %subtract_subtract_fusion, f32[2,1024,1]{1,0,2:T(2,128)S(1)} %bitcast.1325), kind=kOutput, calls=%fused_computation.977 | convolution fusion | flops 50331648 | bytes 16801792 | tf_op jit(solution)/shard_map/mrc,mr->mc/dot_general | solution.py:16
  994.0 33.4 %all-reduce.9 = (f32[2,2048]{1,0:T(2,128)S(1)}, f32[2,6]{1,0:T(2,128)S(1)}, f32[2,6]{1,0:T(2,128)S(1)}, f32[2]{0:T(128)S(1)}, f32[2]{0:T(128)S(1)}, /*index=5*/f...) all-reduce(f32[2,2048]{1,0:T(2,128)S(1)} %bitcast.1344, ...), channel_id=1, replica_groups=mesh['row'=8,'col'=4] {'row'}, use_global_device_ids=true, to_apply=%region_223.224 | all-reduce | flops 8244 | bytes 65952 | tf_op jit(solution)/shard_map/psum | solution.py:57
  1030.5 17.6 %fusion.436 = f32[2,1,1024]{2,1,0:T(1,128)S(1)} fusion(f32[2,1024,2048]{2,1,0:T(8,128)} %subtract_subtract_fusion, f32[2,2048,1]{1,0,2:T(2,128)S(1)} %bitcast.1292), kind=kOutput, calls=%fused_computation.856 | convolution fusion | flops 50331648 | bytes 16801792 | tf_op jit(solution)/shard_map/mrc,mc->mr/dot_general | solution.py:16
  1048.4 10.4 all-reduce.21
  1063.2 16.0 %fusion.138 = f32[2,1024,2048]{2,1,0:T(8,128)} fusion(f32[2,6,2048]{2,0,1:T(2,128)S(1)} %bitcast_dynamic-update-slice_fusion.1, f32[2,6,1024]{2,0,1:T(2,128)S(1)} %constant_dynamic-update-slice_fusion.1), kind=kOutput, calls=%fused_computation.155 | convolution fusion | flops 301989888 | bytes 16924672 | tf_op jit(solution)/shard_map/mpr,mpc->mrc/dot_general | solution.py:16
  1080.5 22.7 %subtract_select_fusion = f32[2,1024,2048]{2,1,0:T(8,128)} fusion(f32[2,1024,2048]{2,1,0:T(8,128)} %subtract_subtract_fusion, f32[2,1024,2048]{2,1,0:T(8,128)} %fusion.138, pred[1024,2048]{1,0:T(8,128)(4,1)S(1)} %broadcast_and_fusion, f32[2,6,2048]{2,0,1:T(2,128)S(1)} %bitcast_dynamic-update-slice_fusion, f32[2,6,1024]{2,0,1:T(2,128)S(1)} %constant_dynamic-update-slice_fusion), kind=kOutput, calls=%fused_computation | convolution fusion | flops 314572800 | bytes 52576256 | tf_op jit(solution)/shard_map/mpr,mpc->mrc/dot_general | solution.py:16
  1103.2 15.8 %copy.1273 = f32[256,8,8,256]{3,2,1,0:T(8,128)} copy(f32[256,8,8,256]{3,1,2,0:T(8,128)} %bitcast.1270) | data formatting | bytes 33554432
  (511 shorter events, 176.8 us)
where the time goes:
time: 1130 us; the launch traced here: 1120 us
  blocking collectives  554 us (49%)
  matrix products  464 us (41%)
  local copies, waits for them, and re-layouts  50 us (4%)
  other arithmetic  47.2 us (4%)
    dot_general x164, matrix products, contract(): return jnp.einsum(form, left, right, precision=lax.Precision.HIGHEST)  464 us
    psum x12, blocking collectives, panel_merged(): lax.psum((contract('mrc,mr->mc', mats, col_piece), contract('mpr,mr->mp',...  415 us
    psum x12, blocking collectives, panel_merged(): lax.psum((contract('mrc,mc->mr', mats, row_piece), contract('mpc,mc->mp',...  125 us

commit v1 on v0

v1 whole, which is shorter than its diff:
```python
import functools

import jax
import jax.numpy as jnp
from jax import lax
from jax.experimental import pallas as pl
from jax.experimental.pallas import tpu as pltpu
from jax.sharding import PartitionSpec as P

STEPS = 6
PANELS = 2
TOTAL = STEPS * PANELS
SLOTS = 16
LANES = 128
MESH = pl.DeviceIdType.MESH


def reflect(leading, squares):
    length = jnp.sqrt(squares)
    divisor = jnp.maximum(leading + length, 1.0)
    factor = (leading + length) / jnp.maximum(length, 1.0)
    return (divisor, factor, -length)


def peers(axis, count):
    me = lax.axis_index(axis)
    return [(lax.rem(me + d, count), lax.rem(me - d + count, count)) for d in range(1, count)]


def positions(length, tile_len, devices, place):
    ids = lax.broadcasted_iota(jnp.int32, (1, length), 1)
    return ids // tile_len * (devices * tile_len) + place * tile_len + ids % tile_len


def pack(batch):
    lane = lax.broadcasted_iota(jnp.int32, (8, LANES), 1)
    tile = jnp.zeros((8, LANES), jnp.float32)
    groups = 2 * SLOTS // 8
    at = 0
    for dots, picked, squares, leading in batch:
        for column in (dots, picked):
            for g in range(groups):
                tile = jnp.where(lane == at, column[g * 8 : (g + 1) * 8], tile)
                at += 1
        for scalar in (squares, leading):
            tile = jnp.where(lane == at, scalar, tile)
            at += 1
    return tile


def unpack(tile, batch_n):
    groups = 2 * SLOTS // 8
    at = 0
    result = []
    for _ in range(batch_n):
        columns = []
        for _ in range(2):
            columns.append(
                jnp.concatenate([tile[:, at + g : at + g + 1] for g in range(groups)], axis=0)
            )
            at += groups
        result.append((columns[0], columns[1], tile[0:1, at : at + 1], tile[0:1, at + 1 : at + 2]))
        at += 2
    return result


def exchange(axis, count, par, big, small, sems):
    send_sem, recv_sem = sems
    me = lax.axis_index(axis)

    def copies(source, target, at):
        return [
            pltpu.make_async_remote_copy(
                src_ref=ref.at[par, source],
                dst_ref=ref.at[par, source],
                send_sem=send_sem.at[which, at],
                recv_sem=recv_sem.at[par, which, source],
                device_id={axis: target},
                device_id_type=MESH,
            )
            for which, ref in enumerate((big, small))
        ]

    sends = []
    for at, (to, _) in enumerate(peers(axis, count)):
        for copy in copies(me, to, at):
            copy.start()
            sends.append(copy)
    for at, (_, source) in enumerate(peers(axis, count)):
        for copy in copies(source, source, at):
            copy.wait_recv()
    for copy in sends:
        copy.wait_send()


def kernel(
    row_n, col_n, tile_len, mats, vx, yu, bid,
    cols, rows, spread, sums, row_big, row_small, col_big, col_small,
    row_send, row_recv, col_send, col_recv, slab_send, slab_recv,
):
    batch_n, height, width = mats.shape
    row_place = lax.axis_index("row")
    col_place = lax.axis_index("col")
    barrier = pltpu.get_barrier_semaphore()
    for axis, count in (("row", row_n), ("col", col_n)):
        for to, _ in peers(axis, count):
            pl.semaphore_signal(barrier, inc=1, device_id={axis: to}, device_id_type=MESH)
    pl.semaphore_wait(barrier, row_n + col_n - 2)

    def slab_copy(ref, axis, which, to, at):
        return pltpu.make_async_remote_copy(
            src_ref=ref,
            dst_ref=ref,
            send_sem=slab_send.at[which, at],
            recv_sem=slab_recv.at[which],
            device_id={axis: to},
            device_id_type=MESH,
        )

    slabs = (("col", col_n, cols, col_place), ("row", row_n, rows, row_place))

    @pl.when(col_place == 0)
    def _():
        for m in range(batch_n):
            for b in range(height // LANES):
                span = pl.ds(b * LANES, LANES)
                cols[m, :, span] = mats[m, span, 0:LANES].T[0:SLOTS]
        for at in range(1, col_n):
            slab_copy(cols, "col", 0, at, at).start()

    @pl.when(row_place == 0)
    def _():
        for m in range(batch_n):
            rows[m] = mats[m, 0:SLOTS, :]
        for at in range(1, row_n):
            slab_copy(rows, "row", 1, at, at).start()

    vx[...] = jnp.zeros_like(vx)
    yu[...] = jnp.zeros_like(yu)
    bid[...] = jnp.zeros_like(bid)

    @pl.when(col_place != 0)
    def _():
        slab_copy(cols, "col", 0, 0, 0).wait_recv()

    grow = positions(height, tile_len, row_n, row_place)
    gcol = positions(width, tile_len, col_n, col_place)
    slot = lax.broadcasted_iota(jnp.int32, (2 * SLOTS, 1), 0)
    lane = lax.broadcasted_iota(jnp.int32, (1, LANES), 1)
    own_row = jnp.where(row_place == 0, lane, -1)
    own_col = jnp.where(col_place == 0, lane, -1)
    row_at = lax.broadcasted_iota(jnp.int32, (8, LANES), 0)
    lane_at = lax.broadcasted_iota(jnp.int32, (8, LANES), 1)

    def full_sum(value):
        return jnp.sum(value, axis=1, keepdims=True)

    def step_body(step, weighs):
        par = lax.rem(step, 2)
        col_pieces = []
        batch = []
        for m in range(batch_n):
            old = vx[m]
            piece = cols[m, pl.ds(step, 1), :] - jnp.sum(weighs[m] * old, axis=0, keepdims=True)
            piece = jnp.where(grow >= step, piece, 0.0)
            batch.append(
                (
                    full_sum(old * piece),
                    full_sum(jnp.where(own_row == step, old[:, 0:LANES], 0.0)),
                    full_sum(piece * piece),
                    full_sum(jnp.where(grow == step, piece, 0.0)),
                )
            )
            col_pieces.append(piece)
            for b in range(height // LANES):
                span = slice(b * LANES, (b + 1) * LANES)
                spread[m, span, :] = jnp.broadcast_to(piece[:, span], (LANES, LANES)).T
        for m in range(batch_n):

            def add_rows(at, total):
                span = pl.ds(pl.multiple_of(at * 8, 8), 8)
                scale = spread[m, span, :]
                return tuple(
                    total[t] + mats[m, span, t * LANES : (t + 1) * LANES] * scale
                    for t in range(width // LANES)
                )

            zeros = tuple(jnp.zeros((8, LANES), jnp.float32) for _ in range(width // LANES))
            total = lax.fori_loop(0, height // 8, add_rows, zeros, unroll=4)
            row_big[par, row_place, m : m + 1, :] = jnp.concatenate(
                [jnp.sum(t, axis=0, keepdims=True) for t in total], axis=1
            )
        row_small[par, row_place] = pack(batch)
        exchange("row", row_n, par, row_big, row_small, (row_send, row_recv))

        @pl.when((row_place != 0) & (step == 0))
        def _():
            slab_copy(rows, "row", 1, 0, 0).wait_recv()

        small = row_small[par, 0]
        trans = row_big[par, 0]
        for s in range(1, row_n):
            small = small + row_small[par, s]
            trans = trans + row_big[par, s]
        small_list = unpack(small, batch_n)
        row_pieces = []
        batch = []
        marks = bid[...]
        for m in range(batch_n):
            dots, picked, squares, leading = small_list[m]
            divisor, factor, bidiag = reflect(leading, squares)
            marks = jnp.where((row_at == m) & (lane_at == step), bidiag, marks)
            remain = 1.0 - leading / divisor
            vx[m, pl.ds(step, 1), :] = jnp.where(grow == step, 1.0, col_pieces[m] / divisor)
            pivot_row = rows[m, pl.ds(step, 1), :]
            old = yu[m]
            weight = dots / divisor + picked * remain
            image = factor * (
                trans[m : m + 1] / divisor
                + pivot_row * remain
                - jnp.sum(weight * old, axis=0, keepdims=True)
            )
            image = jnp.where(gcol > step, image, 0.0)
            yu[m, pl.ds(step, 1), :] = image
            piece = pivot_row - image - jnp.sum(picked * old, axis=0, keepdims=True)
            piece = jnp.where(gcol > step, piece, 0.0)
            new = yu[m]
            batch.append(
                (
                    full_sum(new * piece),
                    full_sum(jnp.where(own_col == step + 1, new[:, 0:LANES], 0.0)),
                    full_sum(piece * piece),
                    full_sum(jnp.where(gcol == step + 1, piece, 0.0)),
                )
            )
            row_pieces.append(piece)
        for m in range(batch_n):
            piece = row_pieces[m]
            scale = [
                jnp.broadcast_to(piece[:, t * LANES : (t + 1) * LANES], (8, LANES))
                for t in range(width // LANES)
            ]

            @pl.loop(0, height // 8, unroll=4)
            def _(at):
                span = pl.ds(pl.multiple_of(at * 8, 8), 8)
                parts = [
                    mats[m, span, t * LANES : (t + 1) * LANES] * scale[t]
                    for t in range(width // LANES)
                ]
                while len(parts) > 1:
                    parts = [
                        parts[i] + parts[i + 1] if i + 1 < len(parts) else parts[i]
                        for i in range(0, len(parts), 2)
                    ]
                sums[m, span, :] = parts[0]

        for m in range(batch_n):
            for b in range(height // LANES):
                span = slice(b * LANES, (b + 1) * LANES)
                col_big[par, col_place, m : m + 1, span] = jnp.sum(
                    sums[m, span, :].T, axis=0, keepdims=True
                )
        col_small[par, col_place] = pack(batch)
        exchange("col", col_n, par, col_big, col_small, (col_send, col_recv))
        small = col_small[par, 0]
        applied = col_big[par, 0]
        for s in range(1, col_n):
            small = small + col_small[par, s]
            applied = applied + col_big[par, s]
        small_list = unpack(small, batch_n)
        later = []
        for m in range(batch_n):
            dots, picked, squares, leading = small_list[m]
            divisor, factor, bidiag = reflect(leading, squares)
            marks = jnp.where((row_at == m) & (lane_at == step + SLOTS), bidiag, marks)
            remain = 1.0 - leading / divisor
            yu[m, pl.ds(SLOTS + step, 1), :] = jnp.where(
                gcol == step + 1, 1.0, row_pieces[m] / divisor
            )
            weight = dots / divisor + picked * remain
            image = factor * (
                applied[m : m + 1] / divisor
                + cols[m, pl.ds(step + 1, 1), :] * remain
                - jnp.sum(weight * vx[m], axis=0, keepdims=True)
            )
            vx[m, pl.ds(SLOTS + step, 1), :] = jnp.where(grow > step, image, 0.0)
            later.append(jnp.where(slot == SLOTS + step, 1.0, picked))
        bid[...] = marks
        return tuple(later)

    none = tuple(jnp.zeros((2 * SLOTS, 1), jnp.float32) for _ in range(batch_n))
    lax.fori_loop(0, TOTAL, step_body, none)

    for which, (axis, count, ref, place) in enumerate(slabs):

        @pl.when(place == 0)
        def _():
            for at in range(1, count):
                slab_copy(ref, axis, which, at, at).wait_send()


def factor_all(mats, row_n, col_n, tile_len):
    batch_n, height, width = mats.shape
    whole = pl.BlockSpec(memory_space=pltpu.VMEM)
    f32 = jnp.float32
    return pl.pallas_call(
        functools.partial(kernel, row_n, col_n, tile_len),
        out_shape=(
            jax.ShapeDtypeStruct((batch_n, 2 * SLOTS, height), f32),
            jax.ShapeDtypeStruct((batch_n, 2 * SLOTS, width), f32),
            jax.ShapeDtypeStruct((8, LANES), f32),
        ),
        in_specs=[whole],
        out_specs=(whole, whole, whole),
        scratch_shapes=[
            pltpu.VMEM((batch_n, SLOTS, height), f32),
            pltpu.VMEM((batch_n, SLOTS, width), f32),
            pltpu.VMEM((batch_n, height, LANES), f32),
            pltpu.VMEM((batch_n, height, LANES), f32),
            pltpu.VMEM((2, row_n, batch_n, width), f32),
            pltpu.VMEM((2, row_n, 8, LANES), f32),
            pltpu.VMEM((2, col_n, batch_n, height), f32),
            pltpu.VMEM((2, col_n, 8, LANES), f32),
            pltpu.SemaphoreType.DMA((2, row_n)),
            pltpu.SemaphoreType.DMA((2, 2, row_n)),
            pltpu.SemaphoreType.DMA((2, col_n)),
            pltpu.SemaphoreType.DMA((2, 2, col_n)),
            pltpu.SemaphoreType.DMA((2, max(row_n, col_n))),
            pltpu.SemaphoreType.DMA((2,)),
        ],
        compiler_params=pltpu.CompilerParams(
            collective_id=0, has_side_effects=True, vmem_limit_bytes=48 * 1024 * 1024
        ),
    )(mats)


def per_device(weights):
    batch_n, row_cycles, tile_len, col_cycles, _ = weights.shape
    height = row_cycles * tile_len
    width = col_cycles * tile_len
    row_n = lax.axis_size("row")
    col_n = lax.axis_size("col")
    mats = weights.reshape(batch_n, height, width)
    vx, yu, bid = factor_all(mats, row_n, col_n, tile_len)
    grow = positions(height, tile_len, row_n, lax.axis_index("row"))[0]
    gcol = positions(width, tile_len, col_n, lax.axis_index("col"))[0]
    inside = (grow[:, None] >= TOTAL) & (gcol[None, :] >= TOTAL)
    update = jnp.einsum("mpr,mpc->mrc", vx, yu, precision=lax.Precision.HIGH)
    trailing = jnp.where(inside[None], mats - update, 0.0).reshape(weights.shape)
    return (trailing, bid[:batch_n, :TOTAL], bid[:batch_n, SLOTS : SLOTS + TOTAL])


def solution(mesh):
    placed = (P(None, None, "row", None, "col"),)
    return jax.shard_map(
        per_device,
        mesh=mesh,
        in_specs=placed,
        out_specs=(P(None, None, "row", None, "col"), P(), P()),
        check_vma=False,
    )
```

time: 1130 us -> 255 us (0.23)
  blocking collectives: 554 us -> 0 us
  matrix products: 464 us -> 14.8 us
  Pallas kernels: 0 us -> 203 us
  other arithmetic: 47.2 us -> 1.39 us
  local copies, waits for them, and re-layouts: 50 us -> 34.4 us
    psum x26 -> x0, blocking collectives: 554 us -> none  [the longest x12 415 us: panel_merged(): lax.psum((contract('mrc,mr->mc', mats, col_piece), contract('mpr,mr->mp',...]
    dot_general x164 -> x1, matrix products: 464 us -> 14.8 us  [per_device(): update = jnp.einsum('mpr,mpc->mrc', vx, yu, precision=lax.Precision.HIGH)]
    pallas_call x0 -> x1, Pallas kernels: none -> 203 us  [factor_all(): pl.pallas_call(functools.partial(kernel, row_n, col_n, tile_len), out_sha...]
    select_n x56 -> x0, other arithmetic: 20.5 us -> none  [the longest x2 15.9 us: panel_merged(): jnp.where(own_col, mats[:, :, next_local], 0.0)]
    another operation x29 -> x0, other arithmetic: 15.3 us -> none
where the time goes in v1:
time: 255 us; the launch traced here: 254 us
  Pallas kernels  203 us (80%)
  local copies, waits for them, and re-layouts  34.4 us (13%)
  matrix products  14.8 us (6%)
    pallas_call x1, Pallas kernels, factor_all(): pl.pallas_call(functools.partial(kernel, row_n, col_n, tile_len), out_sha...  203 us
    reshape x1, local copies, waits for them, and re-layouts, per_device(): mats = weights.reshape(batch_n, height, width)  18 us
    unnamed x1, local copies, waits for them, and re-layouts  15.8 us
    dot_general x1, matrix products, per_device(): update = jnp.einsum('mpr,mpc->mrc', vx, yu, precision=lax.Precision.HIGH)  14.8 us

profile of v1, /device:TPU:0, one launch (start us, length us, event | category | flops | bytes accessed | tf_op | source)
XLA Modules:
  0.0 254.4 jit_solution(13522067983311633811)
XLA Ops:
  0.7 1.4 broadcast_and_fusion
  2.0 18.0 %reshape.160.mats = f32[2,1024,2048]{2,1,0:T(8,128)} reshape(f32[2,4,256,8,256]{4,3,2,1,0:T(8,128)} %param.1) | data formatting | bytes 33554432 | tf_op jit(solution)/shard_map/reshape | solution.py:344
  20.0 203.2 %shard_map.38 = (f32[2,32,1024]{2,1,0:T(8,128)S(1)}, f32[2,32,2048]{2,1,0:T(8,128)S(1)}, f32[8,128]{1,0:T(8,128)S(1)}) custom-call(f32[2,1024,2048]{2,1,0:T(8,128)} %reshape.160.mats), custom_call_target="tpu_custom_call" | custom-call | tf_op jit(solution)/shard_map/pallas_call | solution.py:307
  223.2 14.8 %subtract_select_fusion = f32[2,1024,2048]{2,1,0:T(8,128)} fusion(f32[2,1024,2048]{2,1,0:T(8,128)} %reshape.160.mats, pred[1024,2048]{1,0:T(8,128)(4,1)S(1)} %broadcast_and_fusion, f32[2,32,1024]{2,1,0:T(8,128)S(1)} %get-tuple-element.6, f32[2,32,2048]{2,1,0:T(8,128)S(1)} %get-tuple-element.7), kind=kOutput, calls=%fused_computation | convolution fusion | flops 813694976 | bytes 36438016 | tf_op jit(solution)/shard_map/mpr,mpc->mrc/dot_general | solution.py:349
  238.0 15.8 %copy.4 = f32[256,8,8,256]{3,2,1,0:T(8,128)} copy(f32[256,8,8,256]{3,1,2,0:T(8,128)} %bitcast.8) | data formatting | bytes 33554432
  253.8 0.6 fusion.22
  (2 shorter events, 0.0 us)
